TPU v7x, 16 devices: a whole 2x2x2 slice. The times are simulated.
16 devices in a mesh: dp: 1, tp: 16 (over x, y, z, core).
Axes of the slice: x: 2, y: 2, z: 2, core: 2. Of those that a mesh axis runs over, the one named last changes fastest.
Arguments:
- x: bfloat16 [2048, 8192], P('dp')
- w_gate: bfloat16 [8192, 49152], P(None, 'tp')
- w_up: bfloat16 [8192, 49152], P(None, 'tp')
- w_down: bfloat16 [49152, 8192], P('tp')
Outputs:
- output: bfloat16 [2048, 8192], P('dp')
All inputs are finite; a program needn't handle non-finite values.
Results may differ from a plain program's by a relative error of at most 0.016.
Values are sent between devices in bfloat16 or wider.
A program may use at most 2 GiB of HBM per device.

v0:
```python
import jax
import jax.numpy as jnp
from jax import lax
from jax.sharding import PartitionSpec as P


def solution(mesh):
    def step(x, w_gate, w_up, w_down):
        gate = jnp.dot(x, w_gate, preferred_element_type=jnp.float32)
        up = jnp.dot(x, w_up, preferred_element_type=jnp.float32)
        hidden = (jax.nn.silu(gate) * up).astype(jnp.bfloat16)
        term = jnp.dot(hidden, w_down, preferred_element_type=jnp.float32).astype(jnp.bfloat16)
        return lax.psum(term, "tp")

    return jax.shard_map(
        step,
        mesh=mesh,
        in_specs=(P("dp", None), P(None, "tp"), P(None, "tp"), P("tp", None)),
        out_specs=P("dp", None),
        check_vma=False,
    )
```

profile of v0, /device:TPU:0, one launch (start us, length us, event | category | flops | bytes accessed | tf_op | source)
XLA Modules:
  0.0 708.4 jit_solution(8995930926195151377)
XLA Ops:
  6.5 0.0 all-reduce.2.cloned.1.call-start
  6.5 116.1 %fusion = f32[2048,3072]{1,0:T(8,128)} fusion(bf16[2048,8192]{1,0:T(8,128)(2,1)} %param.4, bf16[8192,3072]{1,0:T(8,128)(2,1)} %param.5), kind=kOutput, calls=%fused_computation.2 | convolution fusion | flops 103079215104 | bytes 109051904 | tf_op jit(solution)/shard_map/dot_general | solution.py:9
  122.7 121.7 %multiply_convert_fusion = bf16[2048,3072]{1,0:T(8,128)(2,1)} fusion(f32[2048,3072]{1,0:T(8,128)} %fusion, bf16[2048,8192]{1,0:T(8,128)(2,1)} %param.4, bf16[8192,3072]{1,0:T(8,128)(2,1)} %param.6), kind=kOutput, calls=%fused_computation.1 | convolution fusion | flops 103116963840 | bytes 121634816 | tf_op jit(solution)/shard_map/dot_general | solution.py:10
  244.3 114.5 %convolution_convert_fusion = bf16[2048,8192]{1,0:T(8,128)(2,1)} fusion(bf16[2048,3072]{1,0:T(8,128)(2,1)} %multiply_convert_fusion, bf16[3072,8192]{1,0:T(8,128)(2,1)} %param.7), kind=kOutput, calls=%fused_computation | convolution fusion | flops 103095992320 | bytes 96468992 | tf_op jit(solution)/shard_map/dot_general | solution.py:12
  358.9 0.0 all-reduce.2.cloned.1.call-update
  358.9 319.7 %all-reduce.2.cloned.1.call-done = bf16[2048,8192]{1,0:T(8,128)(2,1)} async-done(((bf16[2048,8192]{1,0:T(8,128)(2,1)}), bf16[2048,8192]{1,0:T(8,128)(2,1)}) %all-reduce.2.cloned.1.call-update) | async-done | bytes 33554448 | tf_op jit(solution)/shard_map/psum | solution.py:13
  678.6 23.0 %copy.6 = bf16[2048,8192]{1,0:T(8,128)(2,1)} copy(bf16[2048,8192]{1,0:T(8,128)(2,1)} %all-reduce.2.cloned.1.call-done) | data formatting | bytes 67108864
Async XLA Ops:
  6.5 672.0 %all-reduce.2.cloned.1.call-start = ((), (), s32[]{:S(2)}) async-start(), calls=%async_computation | async-start | bytes 67108864 | tf_op jit(solution)/shard_map/psum | solution.py:13
Sparse Core Ops, SparseCore 0:
  359.0 319.5 all-reduce.1
where the time goes:
time: 709 us; the launch traced here: 708 us
  matrix products  352 us (50%)
  waiting for transfers between devices  320 us (45%)
  local copies, waits for them, and re-layouts  23 us (3%)
  between operations  13.4 us (2%)
    psum x1, waiting for transfers between devices, step(): return lax.psum(term, 'tp')  320 us
    dot_general x1, matrix products, step(): up = jnp.dot(x, w_up, preferred_element_type=jnp.float32)  122 us
    dot_general x1, matrix products, step(): gate = jnp.dot(x, w_gate, preferred_element_type=jnp.float32)  116 us
    dot_general x1, matrix products, step(): jnp.dot(hidden, w_down, preferred_element_type=jnp.float32)  115 us
    unnamed x1, local copies, waits for them, and re-layouts  23 us
  transfers between devices with their start and end apart: 1, of which 1 were waited for; matrix products, arithmetic and copies ran while one was open for 0% of the time, Pallas kernels for 0%

commit v1 on v0

v1 whole, which is shorter than its diff:
```python
import jax
import jax.numpy as jnp
from jax import lax
from jax.experimental import pallas as pl
from jax.experimental.pallas import tpu as pltpu
from jax.sharding import PartitionSpec as P

MESH = pl.DeviceIdType.MESH
BF16, F32 = jnp.bfloat16, jnp.float32

R = 512
H = R // 2
TN = 256
TD = 1024
PIECES = 4
ORDERS = ((8, 4, 2), (4, 2, 8), (2, 8, 4))
TILES = ((6, 5, 5), (5, 6, 5), (5, 5, 6), (6, 5, 5))


def part_columns():
    out, at = [], 0
    for tiles in TILES:
        piece = []
        for t in tiles:
            piece.append((at, t * 128))
            at += t * 128
        out.append(piece)
    return out


COLS = part_columns()


def kernel(
    x, wg, wu, wd, y,
    xb, gb, ub, db, h, acc, oth, r0, out, r1, r2, r3,
    xsem, gsem, usem, dsem, s0s, s0r, ss, rs, lsem,
):
    rows, d = x.shape
    nc = rows // R
    ng = wg.shape[1] // TN
    nd = d // TD
    me = lax.axis_index("tp")
    bit = {m: lax.rem(me // m, 2) for m in (1, 2, 4, 8)}
    peer = {m: me + m - 2 * m * bit[m] for m in (1, 2, 4, 8)}
    core = bit[1]

    def remote(src, dst, ssem, rsem, mask):
        return pltpu.make_async_remote_copy(
            src_ref=src, dst_ref=dst, send_sem=ssem, recv_sem=rsem,
            device_id={"tp": peer[mask]}, device_id_type=MESH,
        )

    def load_x(c):
        own = pl.multiple_of(c * R + core * H, H)
        other = pl.multiple_of(c * R + (1 - core) * H, H)
        return (
            pltpu.make_async_copy(x.at[pl.ds(own, H)], xb.at[pl.ds(0, H)], xsem.at[0]),
            pltpu.make_async_copy(x.at[pl.ds(other, H)], xb.at[pl.ds(H, H)], xsem.at[1]),
        )

    def load_gu(j, slot):
        at = pl.ds(pl.multiple_of(j * TN, TN), TN)
        return (
            pltpu.make_async_copy(wg.at[:, at], gb.at[slot], gsem.at[slot]),
            pltpu.make_async_copy(wu.at[:, at], ub.at[slot], usem.at[slot]),
        )

    def load_d(k, slot):
        at = pl.ds(pl.multiple_of(k * TD, TD), TD)
        return (pltpu.make_async_copy(wd.at[:, at], db.at[slot], dsem.at[slot]),)

    def start(copies):
        for c in copies:
            c.start()

    def wait(copies):
        for c in copies:
            c.wait()

    def stage0(k):
        slot = lax.rem(k, 2)
        return remote(oth, r0.at[slot], s0s.at[slot], s0r.at[slot], 1)

    def finish0(k):
        stage0(k).wait()
        at = pl.ds(pl.multiple_of(k * TD, TD), TD)
        acc[:, at] = acc[:, at] + r0[lax.rem(k, 2)].astype(F32)

    def rows_at(c, order, depth):
        at, size = 0, H
        for m in order[:depth]:
            size //= 2
            at = at + bit[m] * size
        return pl.multiple_of(at, size), pl.multiple_of(c * R + core * H + at, size), size

    def scatter(q, p, stage):
        dst = (r1, r2, r3)[stage - 1]
        at = pl.ds(*COLS[q][p])
        return remote(
            out.at[pl.ds(0, H >> stage), at], dst.at[:, at], ss.at[stage, q, p], rs.at[stage, q, p], ORDERS[p][stage - 1]
        )

    def gather(c, q, p, stage):
        order = ORDERS[p]
        depth = 7 - stage
        _, row, size = rows_at(c, order, depth)
        at = pl.ds(*COLS[q][p])
        dst = y.at[pl.ds(row, size), at]
        src = out.at[pl.ds(0, size), at] if stage == 4 else dst
        return remote(src, dst, ss.at[stage, q, p], rs.at[stage, q, p], order[depth - 1])

    def keep(c, q, p):
        _, row, size = rows_at(c, ORDERS[p], 3)
        at = pl.ds(*COLS[q][p])
        return pltpu.make_async_copy(out.at[pl.ds(0, size), at], y.at[pl.ds(row, size), at], lsem.at[q, p])

    def last(c, q):
        row = pl.multiple_of(c * R + core * H, H)
        at = pl.ds(COLS[q][0][0], sum(w for _, w in COLS[q]))
        piece = y.at[pl.ds(row, H), at]
        return remote(piece, piece, ss.at[7, q, 0], rs.at[7, q, 0], 1)

    def act(c, q, stage):
        if stage <= 4:
            for p in range(3):
                order = ORDERS[p]
                at = pl.ds(*COLS[q][p])
                base, _, size = rows_at(c, order, stage - 1)
                if stage > 1:
                    scatter(q, p, stage - 1).wait()
                got = (None, r1, r2, r3)[stage - 1]
                if stage == 4:
                    out[pl.ds(0, size), at] = (acc[pl.ds(base, size), at] + got[:, at].astype(F32)).astype(BF16)
                    keep(c, q, p).start()
                    gather(c, q, p, 4).start()
                    continue
                half = size // 2
                b = bit[order[stage - 1]]
                give = pl.multiple_of((1 - b) * half, half)
                hold = pl.multiple_of(b * half, half)
                to = pl.ds(0, half)
                sums = acc[pl.ds(pl.multiple_of(base + give, half), half), at]
                if stage == 1:
                    out[to, at] = sums.astype(BF16)
                else:
                    out[to, at] = (sums + got[pl.ds(give, half), at].astype(F32)).astype(BF16)
                scatter(q, p, stage).start()
                if stage > 1:
                    mine = pl.ds(pl.multiple_of(base + hold, half), half)
                    acc[mine, at] = acc[mine, at] + got[pl.ds(hold, half), at].astype(F32)
        elif stage <= 7:
            for p in range(3):
                gather(c, q, p, stage - 1).wait()
                if stage == 5:
                    keep(c, q, p).wait()
                if stage < 7:
                    gather(c, q, p, stage).start()
            if stage == 7:
                last(c, q).start()
        else:
            last(c, q).wait()

    def round_(c, n):
        for q in range(PIECES):
            stage = 4 - q + n
            if 1 <= stage <= 8:
                act(c, q, stage)

    barrier = pltpu.get_barrier_semaphore()
    for m in (1, 2, 4, 8):
        pl.semaphore_signal(barrier, inc=1, device_id={"tp": peer[m]}, device_id_type=MESH)
    start(load_x(0))
    start(load_gu(0, 0))
    pl.semaphore_wait(barrier, 4)

    ROUNDS = {1: 1, 3: 2, 5: 3, 7: 4, 9: 5, 10: 6}

    def chunk(c, _):
        wait(load_x(c))

        def gate_up(j, _):
            slot = lax.rem(j, 2)

            @pl.when(j < ng - 1)
            def _():
                start(load_gu(j + 1, 1 - slot))

            @pl.when(j == 0)
            def _():
                start(load_d(0, 0))

            wait(load_gu(j, slot))
            gate = jnp.dot(xb[...], gb[slot], preferred_element_type=F32)
            up = jnp.dot(xb[...], ub[slot], preferred_element_type=F32)
            h[:, pl.ds(pl.multiple_of(j * TN, TN), TN)] = (jax.nn.silu(gate) * up).astype(BF16)

            for step, n in ROUNDS.items():
                @pl.when((c > 0) & (j == step))
                def _():
                    round_(c - 1, n)
            return 0

        lax.fori_loop(0, ng, gate_up, 0)

        def down(k, _):
            slot = lax.rem(k, 2)

            @pl.when(k < nd - 1)
            def _():
                start(load_d(k + 1, 1 - slot))

            @pl.when((k == 0) & (c < nc - 1))
            def _():
                start(load_gu(0, 0))
                start(load_x(c + 1))

            wait(load_d(k, slot))
            term = jnp.dot(h[...], db[slot], preferred_element_type=F32)

            @pl.when(k > 0)
            def _():
                finish0(k - 1)

            acc[:, pl.ds(pl.multiple_of(k * TD, TD), TD)] = term[:H]
            oth[...] = term[H:].astype(BF16)
            stage0(k).start()

            @pl.when((k == 1) & (c > 0))
            def _():
                round_(c - 1, 7)

            for step, n in ((2, -3), (4, -2), (6, -1)):
                @pl.when(k == step)
                def _():
                    round_(c, n)
            return 0

        lax.fori_loop(0, nd, down, 0)
        finish0(nd - 1)
        round_(c, 0)
        return 0

    lax.fori_loop(0, nc, chunk, 0)
    for n in range(1, 8):
        round_(nc - 1, n)


def solution(mesh):
    def step(x, w_gate, w_up, w_down):
        rows, d = x.shape
        ff = w_gate.shape[1]
        hbm = pl.BlockSpec(memory_space=pl.ANY)
        dma = pltpu.SemaphoreType.DMA
        return pl.pallas_call(
            kernel,
            out_shape=jax.ShapeDtypeStruct((rows, d), BF16),
            in_specs=[hbm] * 4,
            out_specs=hbm,
            scratch_shapes=[
                pltpu.VMEM((R, d), BF16),
                pltpu.VMEM((2, d, TN), BF16),
                pltpu.VMEM((2, d, TN), BF16),
                pltpu.VMEM((2, ff, TD), BF16),
                pltpu.VMEM((R, ff), BF16),
                pltpu.VMEM((H, d), F32),
                pltpu.VMEM((H, TD), BF16),
                pltpu.VMEM((2, H, TD), BF16),
                pltpu.VMEM((H // 2, d), BF16),
                pltpu.VMEM((H // 2, d), BF16),
                pltpu.VMEM((H // 4, d), BF16),
                pltpu.VMEM((H // 8, d), BF16),
                dma((2,)),
                dma((2,)),
                dma((2,)),
                dma((2,)),
                dma((2,)),
                dma((2,)),
                dma((8, PIECES, 3)),
                dma((8, PIECES, 3)),
                dma((PIECES, 3)),
            ],
            compiler_params=pltpu.CompilerParams(
                collective_id=0, has_side_effects=True, vmem_limit_bytes=67_000_000
            ),
        )(x, w_gate, w_up, w_down)

    return jax.shard_map(
        step,
        mesh=mesh,
        in_specs=(P("dp", None), P(None, "tp"), P(None, "tp"), P("tp", None)),
        out_specs=P("dp", None),
        check_vma=False,
    )
```

time: 709 us -> 445 us (0.63)
  Pallas kernels: 0 us -> 422 us
  matrix products: 352 us -> 0 us
  waiting for transfers between devices: 320 us -> 0 us
  between operations: 13.4 us -> 0.01 us
    pallas_call x0 -> x1, Pallas kernels: none -> 422 us  [step(): pl.pallas_call(kernel, out_shape=jax.ShapeDtypeStruct((rows, d), BF16), i...]
    dot_general x3 -> x0, matrix products: 352 us -> none  [the longest x1 122 us: step(): up = jnp.dot(x, w_up, preferred_element_type=jnp.float32)]
    psum x1 -> x0, waiting for transfers between devices: 320 us -> none  [step(): return lax.psum(term, 'tp')]
  transfers between devices with their start and end apart: 1 -> 0, of which waited for: 1 -> 0; matrix products, arithmetic and copies ran while one was open for 0% -> 0% of each run, Pallas kernels for 0% -> 0%
where the time goes in v1:
time: 445 us
  Pallas kernels  422 us (95%)
  local copies, waits for them, and re-layouts  23 us (5%)
    pallas_call x1, Pallas kernels, step(): pl.pallas_call(kernel, out_shape=jax.ShapeDtypeStruct((rows, d), BF16), i...  422 us
    unnamed x1, local copies, waits for them, and re-layouts  23 us

profile of v1, /device:TPU:0, one launch (start us, length us, event | category | flops | bytes accessed | tf_op | source)
XLA Modules:
  0.0 445.1 jit_solution(14205452097342318953)
XLA Ops:
  0.0 422.2 %shard_map.46 = bf16[2048,8192]{1,0:T(8,128)(2,1)} custom-call(bf16[2048,8192]{1,0:T(8,128)(2,1)} %x.1, bf16[8192,3072]{1,0:T(8,128)(2,1)} %wg.1, bf16[8192,3072]{1,0:T(8,128)(2,1)} %wu.1, bf16[3072,8192]{1,0:T(8,128)(2,1)} %wd.1), custom_call_target="tpu_custom_call" | custom-call | tf_op jit(solution)/shard_map/pallas_call | solution.py:255
  422.2 23.0 %copy.6 = bf16[2048,8192]{1,0:T(8,128)(2,1)} copy(bf16[2048,8192]{1,0:T(8,128)(2,1)} %shard_map.46) | data formatting | bytes 67108864

commit v2 on v1

--- a/solution.py
+++ b/solution.py
@@ -12,16 +12,31 @@
 H = R // 2
 TN = 256
 TD = 1024
-PIECES = 4
+PIECES = 8
 ORDERS = ((8, 4, 2), (4, 2, 8), (2, 8, 4))
-TILES = ((6, 5, 5), (5, 6, 5), (5, 5, 6), (6, 5, 5))
+TILES = ((3, 3, 2), (3, 2, 3), (2, 3, 3))
+
+AFTER_DOWN = tuple(
+    tuple((q, s) for s in (4, 3, 2, 1) for q in [k + 1 - 2 * s] if q >= 0) for k in range(PIECES)
+)
+ROUNDS = (
+    ((7, 1), (5, 2), (6, 2), (3, 3), (4, 3), (1, 4), (2, 4), (0, 5)),
+    ((7, 2), (5, 3), (6, 3), (3, 4), (4, 4), (1, 5), (2, 5), (0, 6)),
+    ((7, 3), (5, 4), (6, 4), (3, 5), (4, 5), (1, 6), (2, 6), (0, 7)),
+    ((7, 4), (5, 5), (6, 5), (3, 6), (1, 7), (2, 7), (0, 8)),
+    ((7, 5), (4, 6), (5, 6), (3, 7), (1, 8), (2, 8)),
+    ((7, 6), (6, 6), (4, 7), (5, 7), (3, 8)),
+    ((7, 7), (6, 7), (4, 8), (5, 8)),
+    ((6, 8), (7, 8)),
+)
+AFTER_GATE_UP = (0, 2, 4, 6, 8, 10, 11)
 
 
 def part_columns():
     out, at = [], 0
-    for tiles in TILES:
+    for q in range(PIECES):
         piece = []
-        for t in tiles:
+        for t in TILES[q % 3]:
             piece.append((at, t * 128))
             at += t * 128
         out.append(piece)
@@ -80,7 +95,7 @@
 
     def stage0(k):
         slot = lax.rem(k, 2)
-        return remote(oth, r0.at[slot], s0s.at[slot], s0r.at[slot], 1)
+        return remote(oth.at[slot], r0.at[slot], s0s.at[slot], s0r.at[slot], 1)
 
     def finish0(k):
         stage0(k).wait()
@@ -161,11 +176,9 @@
         else:
             last(c, q).wait()
 
-    def round_(c, n):
-        for q in range(PIECES):
-            stage = 4 - q + n
-            if 1 <= stage <= 8:
-                act(c, q, stage)
+    def acts(c, pairs):
+        for q, stage in pairs:
+            act(c, q, stage)
 
     barrier = pltpu.get_barrier_semaphore()
     for m in (1, 2, 4, 8):
@@ -174,8 +187,6 @@
     start(load_gu(0, 0))
     pl.semaphore_wait(barrier, 4)
 
-    ROUNDS = {1: 1, 3: 2, 5: 3, 7: 4, 9: 5, 10: 6}
-
     def chunk(c, _):
         wait(load_x(c))
 
@@ -195,10 +206,12 @@
             up = jnp.dot(xb[...], ub[slot], preferred_element_type=F32)
             h[:, pl.ds(pl.multiple_of(j * TN, TN), TN)] = (jax.nn.silu(gate) * up).astype(BF16)
 
-            for step, n in ROUNDS.items():
+            for step, pairs in zip(AFTER_GATE_UP, ROUNDS):
                 @pl.when((c > 0) & (j == step))
                 def _():
-                    round_(c - 1, n)
+                    if step == AFTER_GATE_UP[0]:
+                        finish0(nd - 1)
+                    acts(c - 1, pairs)
             return 0
 
         lax.fori_loop(0, ng, gate_up, 0)
@@ -218,32 +231,33 @@
             wait(load_d(k, slot))
             term = jnp.dot(h[...], db[slot], preferred_element_type=F32)
 
+            acc[:, pl.ds(pl.multiple_of(k * TD, TD), TD)] = term[:H]
+            oth[slot] = term[H:].astype(BF16)
+
             @pl.when(k > 0)
             def _():
                 finish0(k - 1)
 
-            acc[:, pl.ds(pl.multiple_of(k * TD, TD), TD)] = term[:H]
-            oth[...] = term[H:].astype(BF16)
             stage0(k).start()
 
-            @pl.when((k == 1) & (c > 0))
-            def _():
-                round_(c - 1, 7)
-
-            for step, n in ((2, -3), (4, -2), (6, -1)):
-                @pl.when(k == step)
-                def _():
-                    round_(c, n)
+            @pl.when((k == 0) & (c > 0))
+            def _():
+                acts(c - 1, ROUNDS[-1])
+
+            for step, pairs in enumerate(AFTER_DOWN):
+                if pairs:
+                    @pl.when(k == step)
+                    def _():
+                        acts(c, pairs)
             return 0
 
         lax.fori_loop(0, nd, down, 0)
-        finish0(nd - 1)
-        round_(c, 0)
         return 0
 
     lax.fori_loop(0, nc, chunk, 0)
-    for n in range(1, 8):
-        round_(nc - 1, n)
+    finish0(nd - 1)
+    for pairs in ROUNDS:
+        acts(nc - 1, pairs)
 
 
 def solution(mesh):
@@ -264,7 +278,7 @@
                 pltpu.VMEM((2, ff, TD), BF16),
                 pltpu.VMEM((R, ff), BF16),
                 pltpu.VMEM((H, d), F32),
-                pltpu.VMEM((H, TD), BF16),
+                pltpu.VMEM((2, H, TD), BF16),
                 pltpu.VMEM((2, H, TD), BF16),
                 pltpu.VMEM((H // 2, d), BF16),
                 pltpu.VMEM((H // 2, d), BF16),

time: 445 us -> 428 us (0.962)
  Pallas kernels: 422 us -> 404 us
    pallas_call x1, Pallas kernels: 422 us -> 404 us  [step(): pl.pallas_call(kernel, out_shape=jax.ShapeDtypeStruct((rows, d), BF16), i...]
where the time goes in v2:
time: 428 us; the launch traced here: 427 us
  Pallas kernels  404 us (94%)
  local copies, waits for them, and re-layouts  23 us (5%)
    pallas_call x1, Pallas kernels, step(): pl.pallas_call(kernel, out_shape=jax.ShapeDtypeStruct((rows, d), BF16), i...  404 us
    unnamed x1, local copies, waits for them, and re-layouts  23 us

profile of v2, /device:TPU:0, one launch (start us, length us, event | category | flops | bytes accessed | tf_op | source)
XLA Modules:
  0.0 427.5 jit_solution(15523826198565817896)
XLA Ops:
  0.0 404.5 %shard_map.46 = bf16[2048,8192]{1,0:T(8,128)(2,1)} custom-call(bf16[2048,8192]{1,0:T(8,128)(2,1)} %x.1, bf16[8192,3072]{1,0:T(8,128)(2,1)} %wg.1, bf16[8192,3072]{1,0:T(8,128)(2,1)} %wu.1, bf16[3072,8192]{1,0:T(8,128)(2,1)} %wd.1), custom_call_target="tpu_custom_call" | custom-call | tf_op jit(solution)/shard_map/pallas_call | solution.py:269
  404.5 23.0 %copy.6 = bf16[2048,8192]{1,0:T(8,128)(2,1)} copy(bf16[2048,8192]{1,0:T(8,128)(2,1)} %shard_map.46) | data formatting | bytes 67108864
